TPU v7x, 32 devices: a whole 2x2x4 slice. The times are simulated.
32 devices in a mesh: view: 4 (over x, core), depth: 8 (over z, y).
Axes of the slice: x: 2, y: 2, z: 4, core: 2. Of those that a mesh axis runs over, the one named last changes fastest.
Arguments:
- volume: float32 [128, 128, 512], P(('view', 'depth')), may hold values from -6 to 6
- step_weights: float32 [4, 8, 64], P('view'), may hold values from -0.75 to 0.75
- row_interp: float32 [4, 64, 64], P('view'), may hold values from -0.75 to 0.75
- col_interp: float32 [4, 64, 64], P('view'), may hold values from -0.75 to 0.75
- tf_table: float32 [8, 8], replicated, may hold values from -3 to 3
- materials: int32 [2, 2, 8], P(None, None, 'depth'), may hold values from 0 to 7
- entry: int32 [4, 128, 128], P('view'), may hold values from 0 to 3
Outputs:
- picture: float32 [4, 3, 128, 128], P('view', None, 'depth')
All inputs are finite; a program needn't handle non-finite values.
Results may differ from a plain program's by a relative error of at most 0.00018.
Values sent between devices are 32-bit elements; how exact they have to be, the bound alone decides.
No kernel may reach another device: no remote copies, remote signals or barrier semaphores. Data moves between devices by JAX's collectives and lax.ppermute only.
A program may use at most 64 MiB of HBM per device.

v0:
```python
import jax
import jax.numpy as jnp
from jax import lax
from jax.sharding import PartitionSpec as P


def prefix(part, axis, combine, identity):
    place = lax.axis_index(axis)
    gathered = lax.all_gather(part, axis)
    state = jnp.zeros_like(part) + jnp.asarray(identity, part.dtype)

    def one(lap, state):
        return combine(state, lax.dynamic_index_in_dim(gathered, lap, 0, False))

    return lax.fori_loop(0, place, one, state)


def finish_brick(first, rows_map, cols_map):
    highest = lax.Precision.HIGHEST
    edge = rows_map.shape[0]
    count_steps, total_rows, total_cols = first.shape
    second = first.reshape(count_steps, total_rows // edge, edge, total_cols)
    second = jnp.einsum("stky,rk->stry", second, rows_map, precision=highest)
    third = second.reshape(count_steps, total_rows, total_cols // edge, edge)
    third = jnp.einsum("szuj,cj->szuc", third, cols_map, precision=highest)
    return third.reshape(count_steps, total_rows, total_cols)


def expand_classes(classes, tf_table, edge):
    choices_range = jnp.arange(tf_table.shape[0], dtype=jnp.int32)
    onehot = (classes[:, :, None] == choices_range).astype(jnp.float32)
    tiles = jnp.einsum("abm,mc->cab", onehot, tf_table, precision=lax.Precision.HIGHEST)
    count_coef, tiles_rows, tiles_cols = tiles.shape
    spread = jnp.broadcast_to(
        tiles[:, :, None, :, None], (count_coef, tiles_rows, edge, tiles_cols, edge)
    )
    return spread.reshape(count_coef, tiles_rows * edge, tiles_cols * edge)


def shade(samples, coefficients, live_mask, step_length):
    emission = jax.nn.softplus(coefficients[0:3, None] * samples[None] + coefficients[3:6, None])
    tau = (
        step_length
        * live_mask[None]
        * jax.nn.softplus(coefficients[6][None] * samples + coefficients[7][None])
    )
    earlier = jnp.cumsum(tau, axis=0) - tau
    weights = jnp.exp(-earlier) * (1.0 - jnp.exp(-tau))
    colours = jnp.sum(weights[None] * emission, axis=1)
    passed = jnp.exp(-jnp.sum(tau, axis=0))
    return (colours, passed)


def multiply(earlier, later):
    return earlier * later


def shards(volume, step_weights, row_interp, col_interp, tf_table, materials, entry):
    view_count = lax.axis_size("view")
    depth_count = lax.axis_size("depth")
    depth_index = lax.axis_index("depth")
    planes, lateral, span_cells = volume.shape
    brick_edge = span_cells // depth_count
    all_weights = lax.all_gather(step_weights, "view", axis=0, tiled=True)
    count_steps = all_weights.shape[1]
    cells = volume.reshape(planes, lateral, depth_count, brick_edge)
    contracted = jnp.einsum("zybi,gsi->gbszy", cells, all_weights, precision=lax.Precision.HIGHEST)
    contracted = contracted.reshape(view_count * depth_count, count_steps, planes, lateral)
    received = lax.all_to_all(
        contracted, ("view", "depth"), split_axis=0, concat_axis=2, tiled=True
    )
    samples = finish_brick(received[0], row_interp[0], col_interp[0])
    coefficients = expand_classes(materials[:, :, 0], tf_table, brick_edge)
    live_mask = (entry[0] <= depth_index).astype(jnp.float32)
    step_length = 2.0 / (samples.shape[0] * depth_count)
    colours, passed = shade(samples, coefficients, live_mask, step_length)
    before = prefix(passed, "depth", multiply, jnp.ones_like(passed))
    terms = before[None] * colours
    rows_part = lax.psum_scatter(terms, "depth", scatter_dimension=1, tiled=True)
    return rows_part[None]


def solution(mesh):
    placed = (
        P(("view", "depth"), None, None),
        P("view", None, None),
        P("view", None, None),
        P("view", None, None),
        P(),
        P(None, None, "depth"),
        P("view", None, None),
    )
    return jax.shard_map(
        shards,
        mesh=mesh,
        in_specs=placed,
        out_specs=P("view", None, "depth", None),
        check_vma=False,
    )
```

profile of v0, /device:TPU:0, one launch (start us, length us, event | category | flops | bytes accessed | tf_op | source)
XLA Modules:
  0.0 142.9 jit_solution(2641212617554178664)
XLA Ops:
  6.5 0.0 copy-start
  6.5 6.5 %all_gather.7 = f32[4,8,64]{2,1,0:T(8,128)S(1)} all-gather(f32[1,8,64]{2,1,0:T(8,128)} %param.10), channel_id=1, replica_groups=mesh['view'=4,'depth'=8] {'view'}, dimensions={0}, use_global_device_ids=true | all-gather | bytes 10240 | tf_op jit(solution)/shard_map/all_gather | solution.py:64
  13.0 1.5 %copy.50 = f32[4,128,512]{1,2,0:T(8,128)S(1)} copy(f32[4,128,512]{2,1,0:T(8,128)} %param.9) | data formatting | bytes 2097152 | tf_op args[0]
  14.6 0.6 convolution_bitcast_fusion.1
  15.2 0.0 copy-start.3
  15.2 0.0 copy-start.4
  15.2 0.0 copy-start.1
  15.3 0.9 copy.51
  16.1 6.3 %all-to-all-start = ((f32[32,8,4,128]{3,1,2,0:T(8,128)}), f32[32,8,4,128]{3,1,2,0:T(8,128)S(1)}, u32[]{:S(2)}, u32[]{:S(2)}) async-start(f32[32,8,4,128]{3,1,2,0:T(8,128)} %bitcast.10), calls=%async_computation | async-start | bytes 1048576 | tf_op jit(solution)/shard_map/all_to_all | solution.py:69
  22.4 0.0 reduce-scatter.2.cloned.1.call-start
  22.5 0.0 copy-done.3
  22.5 0.0 copy-done.4
  22.5 0.2 convolution_bitcast_fusion.2
  22.7 0.1 fusion.31
  22.8 0.1 copy.59
  22.9 0.1 fusion.30
  22.9 0.1 copy.65
  23.0 0.1 copy.66
  23.1 0.1 broadcast_in_dim.39
  23.2 0.1 broadcast_in_dim.40
  23.3 0.1 broadcast_in_dim.37
  23.4 0.1 broadcast_in_dim.38
  23.4 0.1 copy.61
  23.5 0.0 copy-done.1
  23.6 0.1 copy.48
  23.7 0.1 broadcast_in_dim.41
  23.8 0.1 broadcast_in_dim.42
  23.9 0.1 broadcast_in_dim.43
  24.0 0.1 broadcast_in_dim.44
  24.1 0.2 broadcast_in_dim.46
  24.3 0.2 add.65
  24.5 0.2 broadcast_in_dim.45
  24.7 0.0 copy-start.2
  24.7 0.2 mul.110
  25.0 13.6 %all-to-all-done = f32[32,8,4,128]{3,1,2,0:T(8,128)S(1)} async-done(((f32[32,8,4,128]{3,1,2,0:T(8,128)}), f32[32,8,4,128]{3,1,2,0:T(8,128)S(1)}, u32[]{:S(2)}, u32[]{:S(2)}) %all-to-all-start) | async-done | bytes 524320 | tf_op jit(solution)/shard_map/all_to_all | solution.py:69
  38.6 0.1 copy.52
  38.8 0.0 copy-done.2
  38.8 0.6 convolution_bitcast_fusion
  39.4 0.6 reshape.101
  40.0 0.0 copy-done
  40.0 1.3 fusion.21
  41.4 0.4 multiply_reduce_fusion
  41.8 0.1 copy.55
  41.9 0.2 copy.60
  42.1 0.5 fusion.4
  42.6 0.2 copy.58
  42.8 31.4 %all_gather.8 = f32[8,128,128]{2,1,0:T(8,128)S(1)} all-gather(f32[1,128,128]{2,1,0:T(8,128)S(1)} %copy.55), channel_id=1, replica_groups=mesh['view'=4,'depth'=8] {'depth'}, dimensions={0}, use_global_device_ids=true | all-gather | bytes 589824 | tf_op jit(solution)/shard_map/all_gather | solution.py:9
  74.2 1.0 fusion.1
  75.2 0.7 broadcast_multiply_fusion
  75.9 0.0 reduce-scatter.2.cloned.1.call-update
  75.9 60.1 %reduce-scatter.2.cloned.1.call-done = f32[3,16,128]{2,1,0:T(8,128)} async-done(((f32[3,128,128]{2,1,0:T(8,128)}), f32[3,16,128]{2,1,0:T(8,128)}) %reduce-scatter.2.cloned.1.call-update) | async-done | bytes 24592 | tf_op jit(solution)/shard_map/reduce_scatter | solution.py:79
  (5 shorter events, 0.0 us)
Async XLA Ops:
  6.5 33.5 %copy-start = (f32[1,64,64]{2,1,0:T(8,128)S(1)}, f32[1,64,64]{2,1,0:T(8,128)}, u32[]{:S(2)}) copy-start(f32[1,64,64]{2,1,0:T(8,128)} %param.12) | copy-start | bytes 49156
  15.2 7.2 %copy-start.3 = (f32[8,8]{1,0:T(8,128)S(1)}, f32[8,8]{1,0:T(8,128)}, u32[]{:S(2)}) copy-start(f32[8,8]{1,0:T(8,128)} %param.13) | copy-start | bytes 772
  15.2 7.2 %copy-start.4 = (s32[2,2,1]{1,2,0:T(1,128)S(1)}, s32[2,2,1]{1,2,0:T(1,128)}, u32[]{:S(2)}) copy-start(s32[2,2,1]{1,2,0:T(1,128)} %param.14) | copy-start | bytes 52
  15.2 8.3 %copy-start.1 = (s32[1,128,128]{2,1,0:T(8,128)S(1)}, s32[1,128,128]{2,1,0:T(8,128)}, u32[]{:S(2)}) copy-start(s32[1,128,128]{2,1,0:T(8,128)} %param.15) | copy-start | bytes 196612
  16.1 22.5 %all-to-all-start = ((f32[32,8,4,128]{3,1,2,0:T(8,128)}), f32[32,8,4,128]{3,1,2,0:T(8,128)S(1)}, u32[]{:S(2)}, u32[]{:S(2)}) async-start(f32[32,8,4,128]{3,1,2,0:T(8,128)} %bitcast.10), calls=%async_computation | async-start | bytes 1048576 | tf_op jit(solution)/shard_map/all_to_all | solution.py:69
  22.4 113.6 %reduce-scatter.2.cloned.1.call-start = ((), (), s32[]{:S(2)}) async-start(), calls=%async_computation.2 | async-start | bytes 221184 | tf_op jit(solution)/shard_map/reduce_scatter | solution.py:79
  24.7 14.1 %copy-start.2 = (f32[1,64,64]{2,1,0:T(8,128)S(1)}, f32[1,64,64]{2,1,0:T(8,128)}, u32[]{:S(2)}) copy-start(f32[1,64,64]{2,1,0:T(8,128)} %param.11) | copy-start | bytes 49156
Sparse Core Ops, SparseCore 0:
  76.0 59.9 reduce-scatter.1
where the time goes:
time: 143 us
  waiting for transfers between devices  73.8 us (52%)
  blocking collectives  37.9 us (27%)
  between operations  13.6 us (10%)
  starting transfers between devices  6.33 us (4%)
  local copies, waits for them, and re-layouts  5.89 us (4%)
  matrix products  2.78 us (2%)
  other arithmetic  2.59 us (2%)
    reduce_scatter x1, waiting for transfers between devices, shards(): lax.psum_scatter(terms, 'depth', scatter_dimension=1, tiled=True)  60.1 us
    all_gather x1, blocking collectives, prefix(): gathered = lax.all_gather(part, axis)  31.4 us
    all_to_all x1, waiting for transfers between devices, shards(): lax.all_to_all(contracted, ('view', 'depth'), split_axis=0, concat_axis=2...  13.6 us
    all_gather x1, blocking collectives, shards(): all_weights = lax.all_gather(step_weights, 'view', axis=0, tiled=True)  6.49 us
    all_to_all x1, starting transfers between devices, shards(): lax.all_to_all(contracted, ('view', 'depth'), split_axis=0, concat_axis=2...  6.29 us
  transfers between devices with their start and end apart: 2, of which 2 were waited for; matrix products, arithmetic and copies ran while one was open for 2% of the time, Pallas kernels for 0%

commit v1 on v0

--- a/solution.py
+++ b/solution.py
@@ -66,9 +66,10 @@
     cells = volume.reshape(planes, lateral, depth_count, brick_edge)
     contracted = jnp.einsum("zybi,gsi->gbszy", cells, all_weights, precision=lax.Precision.HIGHEST)
     contracted = contracted.reshape(view_count * depth_count, count_steps, planes, lateral)
-    received = lax.all_to_all(
-        contracted, ("view", "depth"), split_axis=0, concat_axis=2, tiled=True
-    )
+    size = lax.axis_size(("view", "depth"))
+    blocks = jnp.stack(jnp.split(contracted, size, axis=0), axis=0)
+    blocks = lax.all_to_all(blocks, ("view", "depth"), split_axis=0, concat_axis=0)
+    received = jnp.concatenate(blocks, axis=2)
     samples = finish_brick(received[0], row_interp[0], col_interp[0])
     coefficients = expand_classes(materials[:, :, 0], tf_table, brick_edge)
     live_mask = (entry[0] <= depth_index).astype(jnp.float32)

time: 143 us -> 161 us (1.13)
  local copies, waits for them, and re-layouts: 5.89 us -> 24.3 us
    unnamed x12 -> x45, local copies, waits for them, and re-layouts: 1.67 us -> 20.3 us
where the time goes in v1:
time: 161 us
  waiting for transfers between devices  73.9 us (46%)
  blocking collectives  37.6 us (23%)
  local copies, waits for them, and re-layouts  24.3 us (15%)
  between operations  13.6 us (8%)
  starting transfers between devices  6.33 us (4%)
  matrix products  2.77 us (2%)
  other arithmetic  2.59 us (2%)
    reduce_scatter x1, waiting for transfers between devices, shards(): lax.psum_scatter(terms, 'depth', scatter_dimension=1, tiled=True)  60.2 us
    all_gather x1, blocking collectives, prefix(): gathered = lax.all_gather(part, axis)  31.4 us
    unnamed x45, local copies, waits for them, and re-layouts  20.3 us
    all_to_all x1, waiting for transfers between devices, shards(): lax.all_to_all(blocks, ('view', 'depth'), split_axis=0, concat_axis=0)  13.6 us
    all_to_all x1, starting transfers between devices, shards(): lax.all_to_all(blocks, ('view', 'depth'), split_axis=0, concat_axis=0)  6.29 us
    all_gather x1, blocking collectives, shards(): all_weights = lax.all_gather(step_weights, 'view', axis=0, tiled=True)  6.24 us
  transfers between devices with their start and end apart: 2, of which 2 were waited for; matrix products, arithmetic and copies ran while one was open for 2% of the time, Pallas kernels for 0%

profile of v1, /device:TPU:0, one launch (start us, length us, event | category | flops | bytes accessed | tf_op | source)
XLA Modules:
  0.0 161.2 jit_solution(16022445522695697004)
XLA Ops:
  6.5 1.6 copy.81
  8.1 6.2 %all_gather.7 = f32[4,8,64]{2,1,0:T(8,128)S(1)} all-gather(f32[1,8,64]{2,1,0:T(8,128)S(1)} %copy-done.3), channel_id=1, replica_groups=mesh['view'=4,'depth'=8] {'view'}, dimensions={0}, use_global_device_ids=true | all-gather | bytes 10240 | tf_op jit(solution)/shard_map/all_gather | solution.py:64
  14.4 0.6 convolution_bitcast_fusion.1
  15.1 0.6 constant_dynamic-update-slice_fusion.31
  15.7 0.6 constant_dynamic-update-slice_fusion.30
  16.3 0.6 constant_dynamic-update-slice_fusion.29
  16.9 0.6 constant_dynamic-update-slice_fusion.28
  17.5 0.6 constant_dynamic-update-slice_fusion.27
  18.1 0.6 constant_dynamic-update-slice_fusion.26
  18.7 0.6 constant_dynamic-update-slice_fusion.25
  19.3 0.6 constant_dynamic-update-slice_fusion.24
  19.9 0.6 constant_dynamic-update-slice_fusion.23
  20.5 0.6 constant_dynamic-update-slice_fusion.22
  21.1 0.6 constant_dynamic-update-slice_fusion.21
  21.7 0.6 constant_dynamic-update-slice_fusion.20
  22.3 0.6 constant_dynamic-update-slice_fusion.19
  22.9 0.6 constant_dynamic-update-slice_fusion.18
  23.5 0.6 constant_dynamic-update-slice_fusion.17
  24.1 0.6 constant_dynamic-update-slice_fusion.16
  24.7 0.6 constant_dynamic-update-slice_fusion.15
  25.3 0.6 constant_dynamic-update-slice_fusion.14
  25.9 0.6 constant_dynamic-update-slice_fusion.13
  26.5 0.6 constant_dynamic-update-slice_fusion.12
  27.1 0.6 constant_dynamic-update-slice_fusion.11
  27.7 0.6 constant_dynamic-update-slice_fusion.10
  28.3 0.6 constant_dynamic-update-slice_fusion.9
  28.9 0.6 constant_dynamic-update-slice_fusion.8
  29.5 0.6 constant_dynamic-update-slice_fusion.7
  30.1 0.6 constant_dynamic-update-slice_fusion.6
  30.7 0.6 constant_dynamic-update-slice_fusion.5
  31.3 0.6 constant_dynamic-update-slice_fusion.4
  31.9 0.6 constant_dynamic-update-slice_fusion.3
  32.5 0.6 constant_dynamic-update-slice_fusion.2
  33.1 0.6 constant_dynamic-update-slice_fusion.1
  33.7 0.6 constant_dynamic-update-slice_fusion
  34.3 6.3 %all-to-all-start = ((f32[32,1,8,4,128]{4,2,3,1,0:T(8,128)}), f32[32,1,8,4,128]{4,2,3,1,0:T(8,128)S(1)}, u32[]{:S(2)}, u32[]{:S(2)}) async-start(f32[32,1,8,4,128]{4,2,3,1,0:T(8,128)} %constant_dynamic-update-slice_fusion), calls=%async_computation | async-start | bytes 1048576 | tf_op jit(solution)/shard_map/all_to_all | solution.py:71
  40.7 0.2 convolution_bitcast_fusion.2
  41.0 0.1 copy.96
  41.2 0.1 copy.97
  41.5 0.1 copy.79
  41.6 0.1 broadcast_in_dim.41
  41.7 0.1 broadcast_in_dim.42
  41.8 0.1 broadcast_in_dim.43
  41.9 0.1 broadcast_in_dim.44
  42.1 0.1 copy.92
  42.2 0.2 broadcast_in_dim.46
  42.4 0.2 add.65
  42.7 0.1 copy.90
  42.8 0.2 broadcast_in_dim.45
  42.9 0.2 mul.110
  43.2 13.6 %all-to-all-done = f32[32,1,8,4,128]{4,2,3,1,0:T(8,128)S(1)} async-done(((f32[32,1,8,4,128]{4,2,3,1,0:T(8,128)}), f32[32,1,8,4,128]{4,2,3,1,0:T(8,128)S(1)}, u32[]{:S(2)}, u32[]{:S(2)}) %all-to-all-start) | async-done | bytes 524320 | tf_op jit(solution)/shard_map/all_to_all | solution.py:71
  56.8 0.1 copy.83
  57.0 0.6 convolution_bitcast_fusion
  57.6 0.6 reshape.104
  58.2 1.3 fusion.21
  59.6 0.4 multiply_reduce_fusion
  60.0 0.1 copy.86
  60.1 31.4 %all_gather.8 = f32[8,128,128]{2,1,0:T(8,128)S(1)} all-gather(f32[1,128,128]{2,1,0:T(8,128)S(1)} %copy.86), channel_id=1, replica_groups=mesh['view'=4,'depth'=8] {'depth'}, dimensions={0}, use_global_device_ids=true | all-gather | bytes 589824 | tf_op jit(solution)/shard_map/all_gather | solution.py:9
  91.5 0.2 copy.91
  91.7 0.5 fusion.4
  92.2 0.2 copy.89
  92.4 1.0 fusion.1
  93.4 0.7 broadcast_multiply_fusion
  94.1 60.2 %reduce-scatter.2.cloned.1.call-done = f32[3,16,128]{2,1,0:T(8,128)} async-done(((f32[3,128,128]{2,1,0:T(8,128)}), f32[3,16,128]{2,1,0:T(8,128)}) %reduce-scatter.2.cloned.1.call-update) | async-done | bytes 24592 | tf_op jit(solution)/shard_map/reduce_scatter | solution.py:80
  (26 shorter events, 0.6 us)
Async XLA Ops:
  6.5 51.7 %copy-start = (f32[1,64,64]{2,1,0:T(8,128)S(1)}, f32[1,64,64]{2,1,0:T(8,128)}, u32[]{:S(2)}) copy-start(f32[1,64,64]{2,1,0:T(8,128)} %param.12) | copy-start | bytes 49156
  6.5 1.6 copy-start.3
  15.1 25.6 %copy-start.4 = (f32[8,8]{1,0:T(8,128)S(1)}, f32[8,8]{1,0:T(8,128)}, u32[]{:S(2)}) copy-start(f32[8,8]{1,0:T(8,128)} %param.13) | copy-start | bytes 772
  15.1 25.6 %copy-start.5 = (s32[2,2,1]{1,2,0:T(1,128)S(1)}, s32[2,2,1]{1,2,0:T(1,128)}, u32[]{:S(2)}) copy-start(s32[2,2,1]{1,2,0:T(1,128)} %param.14) | copy-start | bytes 52
  16.9 24.6 %copy-start.1 = (s32[1,128,128]{2,1,0:T(8,128)S(1)}, s32[1,128,128]{2,1,0:T(8,128)}, u32[]{:S(2)}) copy-start(s32[1,128,128]{2,1,0:T(8,128)} %param.15) | copy-start | bytes 196612
  34.3 22.5 %all-to-all-start = ((f32[32,1,8,4,128]{4,2,3,1,0:T(8,128)}), f32[32,1,8,4,128]{4,2,3,1,0:T(8,128)S(1)}, u32[]{:S(2)}, u32[]{:S(2)}) async-start(f32[32,1,8,4,128]{4,2,3,1,0:T(8,128)} %constant_dynamic-update-slice_fusion), calls=%async_computation | async-start | bytes 1048576 | tf_op jit(solution)/shard_map/all_to_all | solution.py:71
  40.6 113.7 %reduce-scatter.2.cloned.1.call-start = ((), (), s32[]{:S(2)}) async-start(), calls=%async_computation.2 | async-start | bytes 221184 | tf_op jit(solution)/shard_map/reduce_scatter | solution.py:80
  42.9 14.1 %copy-start.2 = (f32[1,64,64]{2,1,0:T(8,128)S(1)}, f32[1,64,64]{2,1,0:T(8,128)}, u32[]{:S(2)}) copy-start(f32[1,64,64]{2,1,0:T(8,128)} %param.11) | copy-start | bytes 49156
Sparse Core Ops, SparseCore 0:
  94.2 60.0 reduce-scatter.1
